TPU v7x, 32 devices: a whole 2x2x4 slice. The times are simulated.
32 devices in a mesh: samp: 8 (over z, y), gene: 4 (over x, core).
Axes of the slice: x: 2, y: 2, z: 4, core: 2. Of those that a mesh axis runs over, the one named last changes fastest.
Arguments:
- genotypes: int32 [256, 4096], P('samp', 'gene'), may hold values from -2147483648 to 1789569706, as said below
- allele_freq: float32 [4096], P('gene'), may hold values from 0.035 to 0.56
- sample_weight: float32 [16, 256], P(None, 'samp'), may hold values from 0.2 to 2
- residual: float32 [16, 256], P(None, 'samp'), may hold values from -12 to 12
- variant_weight: float32 [4096], P('gene'), may hold values from 0.2 to 4
- block_gene: int32 [32], replicated, may hold values from 0 to 15, as said below
- gene_variants: int32 [16], replicated, may hold values from 1 to 384, as said below
Outputs:
- burden_z: float32 [16], replicated
- skat_z: float32 [16], replicated
Inputs may be any that keep to these rules, and one draw needn't show every extreme that they name: Each word holds 16 dosages 0, 1 or 2: bits 2k and 2k+1 of genotypes[i, v] are the dosage of variant slot v in sample (k, i); a dosage 2 in the top field sets the sign bit. `block_gene`: never falling; the blocks come in aligned groups of four, each shared by two consecutive genes, so every gene has 1 to 3 blocks. `gene_variants`: A gene with m blocks has from (m - 1) * 128 + 1 to m * 128 live variants; the slots after them in its last block are padding.
All inputs are finite; a program needn't handle non-finite values.
Results may differ from a plain program's by a relative error of at most 0.0037.
Values sent between devices are 32-bit elements; how exact they have to be, the bound alone decides.
A program may use at most 64 MiB of HBM per device.

v0:
```python
import jax
import jax.numpy as jnp
from jax import lax
from jax.sharding import PartitionSpec as P

BLK = 128


def unpack(packed_words, allele_part, root_weight):
    fields = root_weight.shape[0]
    offsets = 2 * jnp.arange(fields, dtype=jnp.int32)
    dosage = jnp.bitwise_and(jnp.right_shift(packed_words[None, :, :], offsets[:, None, None]), 3)
    centered = dosage.astype(jnp.float32) - 2.0 * allele_part[None, None, :]
    return (root_weight[:, :, None] * centered).astype(jnp.bfloat16)


def block_grams(scaled, block_count):
    stacked = scaled.reshape(scaled.shape[0] * scaled.shape[1], block_count, BLK)
    return jnp.einsum("sbu,sbv->buv", stacked, stacked, preferred_element_type=jnp.float32)


def block_stats(gram_part, scores, effective):
    weighted_score = effective * scores
    burden_sum = jnp.sum(weighted_score, axis=1)
    skat_sum = jnp.sum(weighted_score * weighted_score, axis=1)
    image = jnp.einsum("buv,bv->bu", gram_part, effective, precision=lax.Precision.HIGHEST)
    burden_var = jnp.sum(effective * image, axis=1)
    diagonal = jnp.diagonal(gram_part, axis1=1, axis2=2)
    trace_one = jnp.sum(effective * effective * diagonal, axis=1)
    scaled_gram = effective[:, :, None] * gram_part * effective[:, None, :]
    trace_two = jnp.sum(scaled_gram * scaled_gram, axis=(1, 2))
    return jnp.stack([burden_sum, burden_var, skat_sum, trace_one, trace_two])


def live_weights(block_ids, variant_part, block_gene, gene_variants):
    total_blocks = block_gene.shape[0]
    genes = gene_variants.shape[0]
    chosen = block_ids[:, None] == jnp.arange(total_blocks, dtype=jnp.int32)[None, :]
    gene_of = jnp.sum(jnp.where(chosen, block_gene[None, :], 0), axis=1)
    first_block = jnp.sum((block_gene[None, :] < gene_of[:, None]).astype(jnp.int32), axis=1)
    member = gene_of[:, None] == jnp.arange(genes, dtype=jnp.int32)[None, :]
    counted = jnp.sum(jnp.where(member, gene_variants[None, :], 0), axis=1)
    column = jnp.arange(BLK, dtype=jnp.int32)
    is_live = (block_ids - first_block)[:, None] * BLK + column[None, :] < counted[:, None]
    return (variant_part * is_live.astype(jnp.float32), member.astype(jnp.float32))


def local(
    genotypes, allele_freq, sample_weight, residual, variant_weight, block_gene, gene_variants
):
    local_blocks = genotypes.shape[1] // BLK
    owned_count = local_blocks // lax.axis_size("samp")
    samp_index = lax.axis_index("samp")
    gene_index = lax.axis_index("gene")
    block_ids = (
        gene_index * local_blocks
        + samp_index * owned_count
        + jnp.arange(owned_count, dtype=jnp.int32)
    )
    variant_blocks = variant_weight.reshape(local_blocks, BLK)
    own_weights = lax.dynamic_slice_in_dim(variant_blocks, samp_index * owned_count, owned_count, 0)
    effective, member = live_weights(block_ids, own_weights, block_gene, gene_variants)
    own_words = lax.all_to_all(genotypes, "samp", split_axis=1, concat_axis=0, tiled=True)
    all_weight, all_residual = (
        lax.all_gather(sample_weight, "samp", axis=1, tiled=True),
        lax.all_gather(residual, "samp", axis=1, tiled=True),
    )
    own_freq = lax.dynamic_slice_in_dim(
        allele_freq, samp_index * owned_count * BLK, owned_count * BLK, 0
    )
    root_all = jnp.sqrt(all_weight)
    weighted_residual = (root_all * all_residual).astype(jnp.bfloat16)
    scaled = unpack(own_words, own_freq, root_all)
    gram_part = block_grams(scaled, owned_count)
    flattened = scaled.reshape(scaled.shape[0] * scaled.shape[1], owned_count * BLK)
    scores = jnp.dot(
        weighted_residual.reshape(1, -1), flattened, preferred_element_type=jnp.float32
    )
    variance = jnp.sum(all_weight * all_residual * all_residual) / (
        all_weight.shape[0] * all_weight.shape[1]
    )
    gene_parts = jnp.dot(
        block_stats(gram_part, scores, effective), member, precision=lax.Precision.HIGHEST
    )
    totals = lax.psum(gene_parts, ("samp", "gene"))
    burden = totals[0] / jnp.sqrt(variance * totals[1])
    skat_score = (totals[2] - variance * totals[3]) / (variance * jnp.sqrt(2.0 * totals[4]))
    return (burden, skat_score)


def solution(mesh):
    placed = (P("samp", "gene"), P("gene"), P(None, "samp"), P(None, "samp"), P("gene"), P(), P())
    return jax.shard_map(local, mesh=mesh, in_specs=placed, out_specs=(P(), P()), check_vma=False)
```

profile of v0, /device:TPU:0, one launch (start us, length us, event | category | flops | bytes accessed | tf_op | source)
XLA Modules:
  0.0 128.4 jit_solution(14625321429608748185)
XLA Ops:
  0.6 0.0 copy-start
  0.6 0.9 copy-done
  1.5 0.6 copy_bitcast_fusion
  2.2 0.0 copy-start.3
  2.2 0.0 copy-start.1
  2.2 7.4 %all-to-all-start = ((s32[32,8,128]{2,0,1:T(8,128)}), s32[32,8,128]{2,0,1:T(8,128)S(1)}, u32[]{:S(2)}, u32[]{:S(2)}) async-start(s32[32,8,128]{2,0,1:T(8,128)} %copy_bitcast_fusion), calls=%async_computation | async-start | bytes 262144 | tf_op jit(solution)/shard_map/all_to_all | solution.py:63
  9.6 0.0 copy-done.3
  9.7 0.6 fusion.16
  10.3 0.6 fusion.19
  10.9 1.3 fusion.17
  12.2 0.0 copy-done.1
  12.2 0.0 copy-start.2
  12.2 31.2 %all-gather.1 = f32[8,32,16]{1,2,0:T(8,128)S(1)} all-gather(f32[1,32,16]{1,2,0:T(8,128)S(1)} %bitcast.67), channel_id=1, replica_groups=mesh['samp'=8,'gene'=4] {'samp'}, dimensions={0}, use_global_device_ids=true | all-gather | bytes 18432 | tf_op jit(solution)/shard_map/all_gather | solution.py:66
  43.4 0.1 reshape.172
  43.5 0.0 copy-done.2
  43.5 30.5 %all-gather = f32[8,32,16]{1,2,0:T(8,128)S(1)} all-gather(f32[1,32,16]{1,2,0:T(8,128)S(1)} %bitcast.68), channel_id=1, replica_groups=mesh['samp'=8,'gene'=4] {'samp'}, dimensions={0}, use_global_device_ids=true | all-gather | bytes 18432 | tf_op jit(solution)/shard_map/all_gather | solution.py:65
  74.1 0.0 copy-start.4
  74.1 0.1 reshape.170
  74.2 0.6 fusion.12
  76.0 0.8 dynamic-slice_multiply_fusion
  76.8 0.0 copy-done.4
  76.8 1.3 fusion.18
  78.1 0.0 all-to-all-done
  78.1 0.1 copy.22
  78.2 0.9 convolution_bitcast_fusion
  79.1 1.2 gather_fusion
  80.4 1.9 %fusion.20 = (f32[]{:T(128)}, f32[1,128]{1,0:T(1,128)S(1)}) fusion(f32[128]{0:T(128)S(1)} %gather_fusion, f32[8,128]{1,0:T(8,128)} %bitcast.70, s32[]{:T(128)S(6)} %select_n.22, s32[]{:T(128)} %fusion.18, s32[]{:T(128)S(6)} %mul.106), kind=kLoop, calls=%fused_computation.37 | loop fusion | flops 767 | bytes 1552 | tf_op jit(solution)/shard_map/reduce_sum | solution.py:29
  82.3 0.8 fusion.11
  83.1 1.2 multiply_reduce_fusion.1
  84.4 0.7 multiply_reduce_fusion
  85.1 3.3 %stack.23 = f32[5,1]{0,1:T(1,128)S(1)} concatenate(f32[1,1]{0,1:T(1,128)} %bitcast.12, f32[1,1]{0,1:T(1,128)} %bitcast.17, f32[1,1]{0,1:T(1,128)} %bitcast.18, f32[1,1]{0,1:T(1,128)} %bitcast.21, f32[1,1]{0,1:T(1,128)} %bitcast.22), dimensions={0} | concatenate | bytes 40 | tf_op jit(solution)/shard_map/stack | solution.py:32
  88.3 0.1 broadcast_multiply_fusion
  88.4 39.5 %psum.7 = f32[5,16]{1,0:T(8,128)S(1)} all-reduce(f32[5,16]{1,0:T(8,128)S(1)} %broadcast_multiply_fusion), channel_id=1, replica_groups=mesh['samp'=8,'gene'=4] {'samp','gene'}, use_global_device_ids=true, to_apply=%region_8.9 | all-reduce | flops 80 | bytes 640 | tf_op jit(solution)/shard_map/psum | solution.py:85
  127.9 0.5 fusion.22
  (4 shorter events, 0.1 us)
Async XLA Ops:
  0.6 0.9 copy-start
  2.2 7.5 %copy-start.3 = (s32[32]{0:T(128)S(1)}, s32[32]{0:T(128)}, u32[]{:S(2)}) copy-start(s32[32]{0:T(128)} %param.12) | copy-start | bytes 388
  2.2 10.0 %copy-start.1 = (f32[16,32]{1,0:T(8,128)S(1)}, f32[16,32]{1,0:T(8,128)}, u32[]{:S(2)}) copy-start(f32[16,32]{1,0:T(8,128)} %param.10) | copy-start | bytes 6148
  2.2 75.9 %all-to-all-start = ((s32[32,8,128]{2,0,1:T(8,128)}), s32[32,8,128]{2,0,1:T(8,128)S(1)}, u32[]{:S(2)}, u32[]{:S(2)}) async-start(s32[32,8,128]{2,0,1:T(8,128)} %copy_bitcast_fusion), calls=%async_computation | async-start | bytes 262144 | tf_op jit(solution)/shard_map/all_to_all | solution.py:63
  12.2 31.3 %copy-start.2 = (f32[16,32]{1,0:T(8,128)S(1)}, f32[16,32]{1,0:T(8,128)}, u32[]{:S(2)}) copy-start(f32[16,32]{1,0:T(8,128)} %param.9) | copy-start | bytes 6148
  74.1 2.7 %copy-start.4 = (s32[16]{0:T(128)S(1)}, s32[16]{0:T(128)}, u32[]{:S(2)}) copy-start(s32[16]{0:T(128)} %param.13) | copy-start | bytes 196
where the time goes:
time: 129 us; the launch traced here: 128 us
  blocking collectives  101 us (78%)
  other arithmetic  8.47 us (7%)
  starting transfers between devices  7.44 us (6%)
  local copies, waits for them, and re-layouts  6.39 us (5%)
  matrix products  2.98 us (2%)
  between operations  1.93 us (1%)
    psum x1, blocking collectives, local(): totals = lax.psum(gene_parts, ('samp', 'gene'))  39.5 us
    all_gather x1, blocking collectives, local(): lax.all_gather(residual, 'samp', axis=1, tiled=True)  31.2 us
    all_gather x1, blocking collectives, local(): lax.all_gather(sample_weight, 'samp', axis=1, tiled=True)  30.5 us
    all_to_all x1, starting transfers between devices, local(): lax.all_to_all(genotypes, 'samp', split_axis=1, concat_axis=0, tiled=True)  7.44 us
    another operation x1, local copies, waits for them, and re-layouts, block_stats(): return jnp.stack([burden_sum, burden_var, skat_sum, trace_one, trace_two])  3.27 us
  transfers between devices with their start and end apart: 1, of which 0 were waited for; matrix products, arithmetic and copies ran while one was open for 4% of the time, Pallas kernels for 0%

commit v1 on v0

--- a/solution.py
+++ b/solution.py
@@ -60,7 +60,15 @@
     variant_blocks = variant_weight.reshape(local_blocks, BLK)
     own_weights = lax.dynamic_slice_in_dim(variant_blocks, samp_index * owned_count, owned_count, 0)
     effective, member = live_weights(block_ids, own_weights, block_gene, gene_variants)
-    own_words = lax.all_to_all(genotypes, "samp", split_axis=1, concat_axis=0, tiled=True)
+    own_words = jnp.concatenate(
+        lax.all_to_all(
+            jnp.stack(jnp.split(genotypes, lax.axis_size("samp"), 1), axis=0),
+            axis_name="samp",
+            split_axis=0,
+            concat_axis=0,
+        ),
+        0,
+    )
     all_weight, all_residual = (
         lax.all_gather(sample_weight, "samp", axis=1, tiled=True),
         lax.all_gather(residual, "samp", axis=1, tiled=True),

time: 129 us -> 138 us (1.070)
  local copies, waits for them, and re-layouts: 6.39 us -> 15.4 us
    unnamed x12 -> x17, local copies, waits for them, and re-layouts: 1.08 us -> 9.39 us
where the time goes in v1:
time: 138 us; the launch traced here: 137 us
  blocking collectives  101 us (73%)
  local copies, waits for them, and re-layouts  15.4 us (11%)
  other arithmetic  8.47 us (6%)
  starting transfers between devices  7.44 us (5%)
  matrix products  2.98 us (2%)
  between operations  1.93 us (1%)
    psum x1, blocking collectives, local(): totals = lax.psum(gene_parts, ('samp', 'gene'))  39.5 us
    all_gather x1, blocking collectives, local(): lax.all_gather(residual, 'samp', axis=1, tiled=True)  31.2 us
    all_gather x1, blocking collectives, local(): lax.all_gather(sample_weight, 'samp', axis=1, tiled=True)  30.5 us
    unnamed x17, local copies, waits for them, and re-layouts  9.39 us
    all_to_all x1, starting transfers between devices, local(): lax.all_to_all(jnp.stack(jnp.split(genotypes, lax.axis_size('samp'), 1),...  7.44 us
    another operation x1, local copies, waits for them, and re-layouts, block_stats(): return jnp.stack([burden_sum, burden_var, skat_sum, trace_one, trace_two])  3.27 us
  transfers between devices with their start and end apart: 1, of which 0 were waited for; matrix products, arithmetic and copies ran while one was open for 4% of the time, Pallas kernels for 0%

profile of v1, /device:TPU:0, one launch (start us, length us, event | category | flops | bytes accessed | tf_op | source)
XLA Modules:
  0.0 137.4 jit_solution(5467603916590996621)
XLA Ops:
  0.6 1.3 constant_dynamic-update-slice_fusion.7
  1.9 1.3 constant_dynamic-update-slice_fusion.6
  3.3 1.3 constant_dynamic-update-slice_fusion.5
  4.6 1.3 constant_dynamic-update-slice_fusion.4
  5.9 1.3 constant_dynamic-update-slice_fusion.3
  7.2 1.3 constant_dynamic-update-slice_fusion.2
  8.5 1.3 constant_dynamic-update-slice_fusion.1
  9.8 1.3 constant_dynamic-update-slice_fusion
  11.2 0.0 copy-start.2
  11.2 0.0 copy-start
  11.2 7.4 %all-to-all-start = ((s32[8,32,128]{2,1,0:T(8,128)}), s32[8,32,128]{2,1,0:T(8,128)S(1)}, u32[]{:S(2)}, u32[]{:S(2)}) async-start(s32[8,32,128]{2,1,0:T(8,128)} %constant_dynamic-update-slice_fusion), calls=%async_computation | async-start | bytes 262144 | tf_op jit(solution)/shard_map/all_to_all | solution.py:64
  18.6 0.0 copy-done.2
  18.6 0.6 fusion.16
  19.3 0.6 fusion.19
  19.9 1.3 fusion.17
  21.2 0.0 copy-done
  21.2 0.0 copy-start.1
  21.2 31.2 %all-gather.1 = f32[8,32,16]{1,2,0:T(8,128)S(1)} all-gather(f32[1,32,16]{1,2,0:T(8,128)S(1)} %bitcast.76), channel_id=1, replica_groups=mesh['samp'=8,'gene'=4] {'samp'}, dimensions={0}, use_global_device_ids=true | all-gather | bytes 18432 | tf_op jit(solution)/shard_map/all_gather | solution.py:74
  52.4 0.1 reshape.168
  52.5 0.0 copy-done.1
  52.5 30.5 %all-gather = f32[8,32,16]{1,2,0:T(8,128)S(1)} all-gather(f32[1,32,16]{1,2,0:T(8,128)S(1)} %bitcast.77), channel_id=1, replica_groups=mesh['samp'=8,'gene'=4] {'samp'}, dimensions={0}, use_global_device_ids=true | all-gather | bytes 18432 | tf_op jit(solution)/shard_map/all_gather | solution.py:73
  83.1 0.0 copy-start.3
  83.1 0.1 reshape.166
  83.2 0.6 fusion.12
  85.0 0.8 dynamic-slice_multiply_fusion
  85.8 0.0 copy-done.3
  85.8 1.3 fusion.18
  87.0 0.0 all-to-all-done
  87.0 0.1 copy.17
  87.1 0.9 convolution_bitcast_fusion
  88.1 1.2 gather_fusion
  89.3 1.9 %fusion.20 = (f32[]{:T(128)}, f32[1,128]{1,0:T(1,128)S(1)}) fusion(f32[128]{0:T(128)S(1)} %gather_fusion, f32[8,128]{1,0:T(8,128)} %bitcast.79, s32[]{:T(128)S(6)} %select_n.22, s32[]{:T(128)} %fusion.18, s32[]{:T(128)S(6)} %mul.106), kind=kLoop, calls=%fused_computation.44 | loop fusion | flops 767 | bytes 1552 | tf_op jit(solution)/shard_map/reduce_sum | solution.py:29
  91.3 0.8 fusion.11
  92.1 1.2 multiply_reduce_fusion.1
  93.3 0.7 multiply_reduce_fusion
  94.0 3.3 %stack.59 = f32[5,1]{0,1:T(1,128)S(1)} concatenate(f32[1,1]{0,1:T(1,128)} %bitcast.19, f32[1,1]{0,1:T(1,128)} %bitcast.24, f32[1,1]{0,1:T(1,128)} %bitcast.25, f32[1,1]{0,1:T(1,128)} %bitcast.28, f32[1,1]{0,1:T(1,128)} %bitcast.29), dimensions={0} | concatenate | bytes 40 | tf_op jit(solution)/shard_map/stack | solution.py:32
  97.3 0.1 broadcast_multiply_fusion
  97.4 39.5 %psum.7 = f32[5,16]{1,0:T(8,128)S(1)} all-reduce(f32[5,16]{1,0:T(8,128)S(1)} %broadcast_multiply_fusion), channel_id=1, replica_groups=mesh['samp'=8,'gene'=4] {'samp','gene'}, use_global_device_ids=true, to_apply=%region_8.9 | all-reduce | flops 80 | bytes 640 | tf_op jit(solution)/shard_map/psum | solution.py:93
  136.9 0.5 fusion.22
  (4 shorter events, 0.1 us)
Async XLA Ops:
  11.2 7.5 %copy-start.2 = (s32[32]{0:T(128)S(1)}, s32[32]{0:T(128)}, u32[]{:S(2)}) copy-start(s32[32]{0:T(128)} %param.12) | copy-start | bytes 388
  11.2 10.0 %copy-start = (f32[16,32]{1,0:T(8,128)S(1)}, f32[16,32]{1,0:T(8,128)}, u32[]{:S(2)}) copy-start(f32[16,32]{1,0:T(8,128)} %param.10) | copy-start | bytes 6148
  11.2 75.9 %all-to-all-start = ((s32[8,32,128]{2,1,0:T(8,128)}), s32[8,32,128]{2,1,0:T(8,128)S(1)}, u32[]{:S(2)}, u32[]{:S(2)}) async-start(s32[8,32,128]{2,1,0:T(8,128)} %constant_dynamic-update-slice_fusion), calls=%async_computation | async-start | bytes 262144 | tf_op jit(solution)/shard_map/all_to_all | solution.py:64
  21.2 31.3 %copy-start.1 = (f32[16,32]{1,0:T(8,128)S(1)}, f32[16,32]{1,0:T(8,128)}, u32[]{:S(2)}) copy-start(f32[16,32]{1,0:T(8,128)} %param.9) | copy-start | bytes 6148
  83.1 2.7 %copy-start.3 = (s32[16]{0:T(128)S(1)}, s32[16]{0:T(128)}, u32[]{:S(2)}) copy-start(s32[16]{0:T(128)} %param.13) | copy-start | bytes 196
